TPU v7x, 32 devices: a whole 2x2x4 slice. The times are simulated.
32 devices in a mesh: dp: 8 (over y, x, core), own: 4 (over z).
Axes of the slice: x: 2, y: 2, z: 4, core: 2. Of those that a mesh axis runs over, the one named last changes fastest.
Arguments:
- grad: bfloat16 [8192, 1024], P(('dp', 'own')), may hold values from -88 to 88
- left_stats: float32 [8, 1024, 1024], P('dp', 'own'), may hold values from -0.4 to 2.6
- right_stats: float32 [8, 1024, 1024], P('dp', 'own'), may hold values from -0.4 to 2.6
- left_roots: float32 [8, 1024, 1024], P('dp', 'own'), may hold values from -0.4 to 2.6, as said below
- right_roots: float32 [8, 1024, 1024], P('dp', 'own'), may hold values from -0.4 to 2.6, as said below
Outputs:
- direction: bfloat16 [8192, 1024], P(('dp', 'own'))
- left_new: float32 [8, 1024, 1024], P('dp', 'own')
- right_new: float32 [8, 1024, 1024], P('dp', 'own')
Inputs may be any that keep to these rules, and one draw needn't show every extreme that they name: `right_roots`: each block's feature-side root is symmetric. `left_roots`: each block's vocabulary-side root is symmetric.
All inputs are finite; a program needn't handle non-finite values.
Results may differ from a plain program's by a relative error of at most 0.0049.
Values may be sent and summed in bfloat16 or wider, within the bound.
No kernel may reach another device: no remote copies, remote signals or barrier semaphores. Data moves between devices by JAX's collectives and lax.ppermute only.
A program may use at most 64 MiB of HBM per device.

v0:
```python
import jax
import jax.numpy as jnp
from jax import lax
from jax.sharding import PartitionSpec as P

highest = lax.Precision.HIGHEST
epsilon = 1e-06


def transpose_product(left_side, right_side):
    return lax.dot_general(
        left_side, right_side, (((0,), (0,)), ((), ())), preferred_element_type=jnp.float32
    )


def local(grad, left_stats, right_stats, left_roots, right_roots):
    feature_width = grad.shape[1]
    owner_count = lax.axis_size("own")
    slice_width = feature_width // owner_count
    own_rows = grad.astype(jnp.float32)
    grad_square = jnp.sum(own_rows * own_rows)
    whole_grad = lax.all_gather(grad, "own", axis=0, tiled=True)
    feature_cols = lax.dynamic_slice_in_dim(
        whole_grad, lax.axis_index("own") * slice_width, slice_width, 1
    )
    left_gram = lax.dot_general(
        grad, whole_grad, (((1,), (1,)), ((), ())), preferred_element_type=jnp.float32
    )
    right_gram = transpose_product(feature_cols, whole_grad)
    left_update = 0.9 * left_stats[0] + 0.1 / feature_width * left_gram
    right_update = 0.9 * right_stats[0] + 0.1 / feature_width * right_gram
    mixed_cols = lax.dot_general(
        whole_grad.astype(jnp.float32), right_roots[0], (((1,), (1,)), ((), ())), precision=highest
    )
    mixed_cols = mixed_cols.astype(jnp.bfloat16)
    precond = jnp.dot(
        left_roots[0],
        lax.all_gather(mixed_cols, "own", axis=1, tiled=True).astype(jnp.float32),
        precision=highest,
    )
    precond_square = jnp.sum(precond * precond)
    norm_totals = lax.psum((grad_square, precond_square), "own")
    graft_scale = jnp.sqrt(norm_totals[0] / (norm_totals[1] + epsilon))
    direction = (precond * graft_scale).astype(jnp.bfloat16)
    return (direction, left_update[None], right_update[None])


def solution(mesh):
    in_specs = (
        P(("dp", "own"), None),
        P("dp", "own", None),
        P("dp", "own", None),
        P("dp", "own", None),
        P("dp", "own", None),
    )
    out_specs = (P(("dp", "own"), None), P("dp", "own", None), P("dp", "own", None))
    return jax.shard_map(local, mesh=mesh, in_specs=in_specs, out_specs=out_specs, check_vma=False)
```

profile of v0, /device:TPU:0, one launch (start us, length us, event | category | flops | bytes accessed | tf_op | source)
XLA Modules:
  0.0 131.7 jit_solution(18139367668326251888)
XLA Ops:
  7.2 0.0 copy-start
  7.2 0.0 all-gather.3.cloned.1.call-start
  7.2 0.7 all-gather.3.cloned.1.call-update
  7.9 0.0 all-gather.5.cloned.1.call-start
  8.0 50.0 %all-gather.3.cloned.1.call-done = bf16[1024,1024]{1,0:T(8,128)(2,1)} async-done(((bf16[256,1024]{1,0:T(8,128)(2,1)}), bf16[1024,1024]{1,0:T(8,128)(2,1)}) %all-gather.3.cloned.1.call-update) | async-done | bytes 2097168 | tf_op jit(solution)/shard_map/all_gather | solution.py:22
  58.0 0.0 copy-start.1
  58.0 4.7 %convolution_convert_fusion = bf16[1024,256]{1,0:T(8,128)(2,1)} fusion(bf16[1024,1024]{1,0:T(8,128)(2,1)} %all-gather.3.cloned.1.call-done, f32[1,256,1024]{2,1,0:T(8,128)} %param.9), kind=kOutput, calls=%fused_computation.6 | convolution fusion | flops 3221487616 | bytes 3670016 | tf_op jit(solution)/shard_map/dot_general | solution.py:32
  62.6 0.0 all-gather.5.cloned.1.call-update
  62.7 1.9 %multiply_reduce_fusion.1 = f32[]{:T(128)} fusion(bf16[256,1024]{1,0:T(8,128)(2,1)} %param.5), kind=kLoop, calls=%fused_computation.12 | loop fusion | flops 786431 | bytes 524292 | tf_op jit(solution)/shard_map/reduce_sum | solution.py:21
  64.6 0.0 copy-done.1
  64.6 0.0 copy-start.2
  64.6 0.0 copy-start.3
  64.6 3.1 %fusion.1 = f32[1,256,1024]{2,1,0:T(8,128)} fusion(bf16[1024,1024]{1,0:T(8,128)(2,1)S(1)} %copy-done.1, f32[1,256,1024]{2,1,0:T(8,128)} %param.7, s32[]{:T(128)S(6)} %select_n.3), kind=kOutput, calls=%fused_computation.2 | convolution fusion | flops 537657344 | bytes 4718596 | tf_op jit(solution)/shard_map/dot_general | solution.py:11
  67.7 0.0 copy-done.2
  67.7 0.0 copy-done.3
  67.7 1.8 %fusion.3 = f32[1,256,1024]{2,1,0:T(8,128)} fusion(bf16[256,1024]{1,0:T(8,128)(2,1)S(1)} %copy-done.2, bf16[1024,1024]{1,0:T(8,128)(2,1)S(1)} %copy-done.1, f32[1,256,1024]{2,1,0:T(8,128)S(1)} %copy-done.3), kind=kOutput, calls=%fused_computation.5 | convolution fusion | flops 537657344 | bytes 4718592 | tf_op jit(solution)/shard_map/dot_general | solution.py:26
  69.4 38.4 %all-gather.5.cloned.1.call-done = bf16[1024,1024]{1,0:T(8,128)(2,1)} async-done(((bf16[1024,256]{1,0:T(8,128)(2,1)}), bf16[1024,1024]{1,0:T(8,128)(2,1)}) %all-gather.5.cloned.1.call-update) | async-done | bytes 2097168 | tf_op jit(solution)/shard_map/all_gather | solution.py:38
  107.9 0.0 copy-done
  107.9 4.6 %multiply_reduce_fusion = (f32[]{:T(128)}, f32[1024,256]{1,0:T(8,128)S(1)}) fusion(bf16[1024,1024]{1,0:T(8,128)(2,1)} %all-gather.5.cloned.1.call-done, f32[1,256,1024]{2,1,0:T(8,128)S(1)} %copy-done), kind=kOutput, calls=%fused_computation.11 | convolution fusion | flops 3221749760 | bytes 4194308 | tf_op jit(solution)/shard_map/dot_general | solution.py:36
  112.4 10.0 %all-reduce = (f32[]{:T(128)}, f32[]{:T(128)}) all-reduce(f32[]{:T(128)} %multiply_reduce_fusion.1, f32[]{:T(128)} %get-tuple-element.8), channel_id=1, replica_groups=mesh['dp'=8,'own'=4] {'own'}, use_global_device_ids=true, to_apply=%region_1.0 | all-reduce | flops 2 | bytes 16 | tf_op jit(solution)/shard_map/psum | solution.py:42
  123.7 0.1 fusion.7
  123.9 1.0 copy.8
Async XLA Ops:
  7.2 100.7 %copy-start = (f32[1,256,1024]{2,1,0:T(8,128)S(1)}, f32[1,256,1024]{2,1,0:T(8,128)}, u32[]{:S(2)}) copy-start(f32[1,256,1024]{2,1,0:T(8,128)} %param.8) | copy-start | bytes 3145732
  7.2 50.8 %all-gather.3.cloned.1.call-start = ((), (), s32[]{:S(2)}) async-start(), calls=%async_computation | async-start | bytes 2621440 | tf_op jit(solution)/shard_map/all_gather | solution.py:22
  7.9 100.0 %all-gather.5.cloned.1.call-start = ((), (), s32[]{:S(2)}) async-start(), calls=%async_computation.1 | async-start | bytes 2621440 | tf_op jit(solution)/shard_map/all_gather | solution.py:38
  58.0 6.6 %copy-start.1 = (bf16[1024,1024]{1,0:T(8,128)(2,1)S(1)}, bf16[1024,1024]{1,0:T(8,128)(2,1)}, u32[]{:S(2)}) copy-start(bf16[1024,1024]{1,0:T(8,128)(2,1)} %all-gather.3.cloned.1.call-done) | copy-start | bytes 6291460
  64.6 3.1 %copy-start.2 = (bf16[256,1024]{1,0:T(8,128)(2,1)S(1)}, bf16[256,1024]{1,0:T(8,128)(2,1)}, u32[]{:S(2)}) copy-start(bf16[256,1024]{1,0:T(8,128)(2,1)} %param.5) | copy-start | bytes 1572868
  64.6 3.1 %copy-start.3 = (f32[1,256,1024]{2,1,0:T(8,128)S(1)}, f32[1,256,1024]{2,1,0:T(8,128)}, u32[]{:S(2)}) copy-start(f32[1,256,1024]{2,1,0:T(8,128)} %param.6) | copy-start | bytes 3145732
Sparse Core Ops, SparseCore 0:
  9.6 48.3 all-gather.2
  62.8 45.0 all-gather.4
where the time goes:
time: 132 us
  waiting for transfers between devices  89.2 us (68%)
  between operations  15.3 us (12%)
  matrix products  14.1 us (11%)
  blocking collectives  10 us (8%)
  other arithmetic  2.01 us (2%)
    all_gather x1, waiting for transfers between devices, local(): whole_grad = lax.all_gather(grad, 'own', axis=0, tiled=True)  50 us
    all_gather x1, waiting for transfers between devices, local(): lax.all_gather(mixed_cols, 'own', axis=1, tiled=True).astype(jnp.float32)  38.4 us
    psum x1, blocking collectives, local(): norm_totals = lax.psum((grad_square, precond_square), 'own')  10 us
    dot_general x1, matrix products, local(): lax.dot_general(whole_grad.astype(jnp.float32), right_roots[0], (((1,), (...  4.66 us
    dot_general x1, matrix products, local(): jnp.dot(left_roots[0], lax.all_gather(mixed_cols, 'own', axis=1, tiled=Tr...  4.57 us
    dot_general x1, matrix products, transpose_product(): lax.dot_general(left_side, right_side, (((0,), (0,)), ((), ())), preferre...  3.07 us
  transfers between devices with their start and end apart: 2, of which 2 were waited for; matrix products, arithmetic and copies ran while one was open for 5% of the time, Pallas kernels for 0%

commit v1 on v0

--- a/solution.py
+++ b/solution.py
@@ -5,6 +5,11 @@
 
 highest = lax.Precision.HIGHEST
 epsilon = 1e-06
+
+
+def all_parts(block, axis, d):
+    blocks = lax.all_gather(block, axis)
+    return jnp.concatenate(blocks, axis=d)
 
 
 def transpose_product(left_side, right_side):
@@ -34,9 +39,7 @@
     )
     mixed_cols = mixed_cols.astype(jnp.bfloat16)
     precond = jnp.dot(
-        left_roots[0],
-        lax.all_gather(mixed_cols, "own", axis=1, tiled=True).astype(jnp.float32),
-        precision=highest,
+        left_roots[0], all_parts(mixed_cols, "own", 1).astype(jnp.float32), precision=highest
     )
     precond_square = jnp.sum(precond * precond)
     norm_totals = lax.psum((grad_square, precond_square), "own")

time: 132 us -> 135 us (1.023)
  local copies, waits for them, and re-layouts: 1.02 us -> 4.01 us
    all_gather x0 -> x1, local copies, waits for them, and re-layouts: none -> 2.99 us  [all_parts(): blocks = lax.all_gather(block, axis)]
where the time goes in v1:
time: 135 us; the launch traced here: 134 us
  waiting for transfers between devices  88.6 us (66%)
  between operations  15.3 us (11%)
  matrix products  12.9 us (10%)
  blocking collectives  10.3 us (8%)
  local copies, waits for them, and re-layouts  4.01 us (3%)
  other arithmetic  3.22 us (2%)
    all_gather x1, waiting for transfers between devices, local(): whole_grad = lax.all_gather(grad, 'own', axis=0, tiled=True)  50 us
    all_gather x1, waiting for transfers between devices, all_parts(): blocks = lax.all_gather(block, axis)  37.8 us
    psum x1, blocking collectives, local(): norm_totals = lax.psum((grad_square, precond_square), 'own')  10.3 us
    dot_general x1, matrix products, local(): lax.dot_general(whole_grad.astype(jnp.float32), right_roots[0], (((1,), (...  4.66 us
    dot_general x1, matrix products, local(): jnp.dot(left_roots[0], all_parts(mixed_cols, 'own', 1).astype(jnp.float32...  3.43 us
    dot_general x1, matrix products, transpose_product(): lax.dot_general(left_side, right_side, (((0,), (0,)), ((), ())), preferre...  3.07 us
    all_gather x1, local copies, waits for them, and re-layouts, all_parts(): blocks = lax.all_gather(block, axis)  2.99 us
  transfers between devices with their start and end apart: 2, of which 2 were waited for; matrix products, arithmetic and copies ran while one was open for 5% of the time, Pallas kernels for 0%

profile of v1, /device:TPU:0, one launch (start us, length us, event | category | flops | bytes accessed | tf_op | source)
XLA Modules:
  0.0 134.5 jit_solution(7012965665412155063)
XLA Ops:
  7.2 0.0 copy-start
  7.2 0.0 all-gather.4.cloned.1.call-start
  7.2 0.7 all-gather.4.cloned.1.call-update
  7.9 0.0 all-gather.6.cloned.1.call-start
  8.0 50.0 %all-gather.4.cloned.1.call-done = bf16[1024,1024]{1,0:T(8,128)(2,1)} async-done(((bf16[256,1024]{1,0:T(8,128)(2,1)}), bf16[1024,1024]{1,0:T(8,128)(2,1)}) %all-gather.4.cloned.1.call-update) | async-done | bytes 2097168 | tf_op jit(solution)/shard_map/all_gather | solution.py:27
  58.0 0.0 copy-start.1
  58.0 4.7 %convolution_convert_fusion = bf16[1024,256]{1,0:T(8,128)(2,1)} fusion(bf16[1024,1024]{1,0:T(8,128)(2,1)} %all-gather.4.cloned.1.call-done, f32[1,256,1024]{2,1,0:T(8,128)} %param.9), kind=kOutput, calls=%fused_computation.6 | convolution fusion | flops 3221487616 | bytes 3670016 | tf_op jit(solution)/shard_map/dot_general | solution.py:37
  62.6 0.0 all-gather.6.cloned.1.call-update
  62.7 1.9 %multiply_reduce_fusion.1 = f32[]{:T(128)} fusion(bf16[256,1024]{1,0:T(8,128)(2,1)} %param.5), kind=kLoop, calls=%fused_computation.12 | loop fusion | flops 786431 | bytes 524292 | tf_op jit(solution)/shard_map/reduce_sum | solution.py:26
  64.6 0.0 copy-done.1
  64.6 0.0 copy-start.2
  64.6 0.0 copy-start.3
  64.6 3.1 %fusion.1 = f32[1,256,1024]{2,1,0:T(8,128)} fusion(bf16[1024,1024]{1,0:T(8,128)(2,1)S(1)} %copy-done.1, f32[1,256,1024]{2,1,0:T(8,128)} %param.7, s32[]{:T(128)S(6)} %select_n.3), kind=kOutput, calls=%fused_computation.2 | convolution fusion | flops 537657344 | bytes 4718596 | tf_op jit(solution)/shard_map/dot_general | solution.py:16
  67.7 0.0 copy-done.2
  67.7 0.0 copy-done.3
  67.7 1.8 %fusion.3 = f32[1,256,1024]{2,1,0:T(8,128)} fusion(bf16[256,1024]{1,0:T(8,128)(2,1)S(1)} %copy-done.2, bf16[1024,1024]{1,0:T(8,128)(2,1)S(1)} %copy-done.1, f32[1,256,1024]{2,1,0:T(8,128)S(1)} %copy-done.3), kind=kOutput, calls=%fused_computation.5 | convolution fusion | flops 537657344 | bytes 4718592 | tf_op jit(solution)/shard_map/dot_general | solution.py:31
  69.4 37.8 %all-gather.6.cloned.1.call-done = bf16[4096,256]{1,0:T(8,128)(2,1)} async-done(((bf16[1024,256]{1,0:T(8,128)(2,1)}), bf16[4096,256]{1,0:T(8,128)(2,1)}) %all-gather.6.cloned.1.call-update) | async-done | bytes 2097168 | tf_op jit(solution)/shard_map/all_gather | solution.py:11
  107.3 3.0 %copy.9 = bf16[4,1024,256]{1,2,0:T(8,128)(2,1)S(1)} copy(bf16[4,1024,256]{2,1,0:T(8,128)(2,1)} %bitcast.28) | data formatting | bytes 4194304 | tf_op jit(solution)/shard_map/all_gather | solution.py:11
  110.3 0.0 copy-done
  110.3 3.4 %multiply_reduce_fusion = (f32[]{:T(128)}, f32[1024,256]{1,0:T(8,128)}) fusion(bf16[1024,1024]{0,1:T(8,128)(2,1)S(1)} %bitcast.27, f32[1,256,1024]{2,1,0:T(8,128)S(1)} %copy-done), kind=kOutput, calls=%fused_computation.11 | convolution fusion | flops 3221749760 | bytes 4194308 | tf_op jit(solution)/shard_map/dot_general | solution.py:41
  113.7 10.3 %all-reduce = (f32[]{:T(128)}, f32[]{:T(128)}) all-reduce(f32[]{:T(128)} %multiply_reduce_fusion.1, f32[]{:T(128)} %get-tuple-element.11), channel_id=1, replica_groups=mesh['dp'=8,'own'=4] {'own'}, use_global_device_ids=true, to_apply=%region_1.0 | all-reduce | flops 2 | bytes 16 | tf_op jit(solution)/shard_map/psum | solution.py:45
  125.3 1.3 fusion.7
  126.6 1.0 copy.10
Async XLA Ops:
  7.2 103.1 %copy-start = (f32[1,256,1024]{2,1,0:T(8,128)S(1)}, f32[1,256,1024]{2,1,0:T(8,128)}, u32[]{:S(2)}) copy-start(f32[1,256,1024]{2,1,0:T(8,128)} %param.8) | copy-start | bytes 3145732
  7.2 50.8 %all-gather.4.cloned.1.call-start = ((), (), s32[]{:S(2)}) async-start(), calls=%async_computation | async-start | bytes 2621440 | tf_op jit(solution)/shard_map/all_gather | solution.py:27
  7.9 99.4 %all-gather.6.cloned.1.call-start = ((), (), s32[]{:S(2)}) async-start(), calls=%async_computation.1 | async-start | bytes 2621440 | tf_op jit(solution)/shard_map/all_gather | solution.py:11
  58.0 6.6 %copy-start.1 = (bf16[1024,1024]{1,0:T(8,128)(2,1)S(1)}, bf16[1024,1024]{1,0:T(8,128)(2,1)}, u32[]{:S(2)}) copy-start(bf16[1024,1024]{1,0:T(8,128)(2,1)} %all-gather.4.cloned.1.call-done) | copy-start | bytes 6291460
  64.6 3.1 %copy-start.2 = (bf16[256,1024]{1,0:T(8,128)(2,1)S(1)}, bf16[256,1024]{1,0:T(8,128)(2,1)}, u32[]{:S(2)}) copy-start(bf16[256,1024]{1,0:T(8,128)(2,1)} %param.5) | copy-start | bytes 1572868
  64.6 3.1 %copy-start.3 = (f32[1,256,1024]{2,1,0:T(8,128)S(1)}, f32[1,256,1024]{2,1,0:T(8,128)}, u32[]{:S(2)}) copy-start(f32[1,256,1024]{2,1,0:T(8,128)} %param.6) | copy-start | bytes 3145732
Sparse Core Ops, SparseCore 0:
  9.6 48.3 all-gather.3
  62.8 44.4 all-gather.5
